TPU v7x, 32 devices: a whole 2x2x4 slice. The times are simulated.
32 devices in a mesh: grp: 8 (over y, x, core), sp: 4 (over z).
Axes of the slice: x: 2, y: 2, z: 4, core: 2. Of those that a mesh axis runs over, the one named last changes fastest.
Arguments:
- latents: bfloat16 [8, 512, 3072], P('grp', 'sp'), may hold values from -6 to 6
- timestep: int32 [8], P('grp'), may hold values from 0 to 999
- w_mod: bfloat16 [256, 9216], replicated, may hold values from -0.375 to 0.375
- w_qkv: bfloat16 [4, 3072, 384], P('sp', 'grp'), may hold values from -2 to 2
- w_out: bfloat16 [4, 128, 3072], P('sp', 'grp'), may hold values from -0.5 to 0.5
Outputs:
- update: bfloat16 [8, 512, 3072], P('grp', 'sp')
All inputs are finite; a program needn't handle non-finite values.
Results may differ from a plain program's by a relative error of at most 0.012.
Values may be sent and summed in bfloat16 or wider, within the bound.
A program may use at most 128 MiB of HBM per device.

v0:
```python
import math
import jax
import jax.numpy as jnp
from jax import lax
from jax.sharding import PartitionSpec as P


def modulation(timestep, w_mod):
    half_freq = w_mod.shape[0] // 2
    freqs = jnp.exp(-math.log(10000.0) * jnp.arange(half_freq, dtype=jnp.float32) / half_freq)
    angles = timestep.astype(jnp.float32)[:, None] * freqs[None, :]
    embed = jnp.concatenate([jnp.cos(angles), jnp.sin(angles)], axis=1).astype(jnp.bfloat16)
    return jnp.dot(embed, w_mod, preferred_element_type=jnp.float32)


def normalize(latents, shift, scale):
    values = latents.astype(jnp.float32)
    center = jnp.mean(values, axis=-1, keepdims=True)
    spread = jnp.mean((values - center) ** 2, axis=-1, keepdims=True)
    normed = (values - center) * lax.rsqrt(spread + 1e-06)
    return (normed * (1.0 + scale[:, None, :]) + shift[:, None, :]).astype(jnp.bfloat16)


def attend(query, keys, values):
    length, head_size = query.shape
    block = min(512, length)
    blocks = query.reshape(length // block, block, head_size)

    def one_block(query_rows):
        scores = lax.dot_general(
            query_rows, keys, (((1,), (1,)), ((), ())), preferred_element_type=jnp.float32
        )
        scores = scores / math.sqrt(head_size)
        largest = jnp.max(scores, axis=1, keepdims=True)
        weights = jnp.exp(scores - largest)
        probs = (weights / jnp.sum(weights, axis=1, keepdims=True)).astype(jnp.bfloat16)
        return jnp.dot(probs, values, preferred_element_type=jnp.float32).astype(jnp.bfloat16)

    return lax.map(one_block, blocks).reshape(length, head_size)


def on_device(latents, timestep, w_mod, w_qkv, w_out):
    images, tok_local, width = latents.shape
    triple = w_qkv.shape[2]
    head_size = triple // 3
    mod = modulation(timestep, w_mod)
    shift = mod[:, :width]
    scale = mod[:, width : 2 * width]
    gate = mod[:, 2 * width :]
    normed = normalize(latents, shift, scale)
    whole = lax.all_gather(normed, "sp", axis=1, tiled=True)
    qkv_sum = jnp.einsum(
        "itc,cf->itf",
        whole,
        lax.all_gather(w_qkv, "grp", axis=1, tiled=True)[0],
        preferred_element_type=jnp.float32,
    )
    qkv = qkv_sum.astype(jnp.bfloat16)
    out_rows = lax.all_gather(w_out, "grp", axis=1, tiled=True)
    attended = jnp.stack(
        [
            attend(
                qkv[0, :, :head_size],
                qkv[0, :, head_size : 2 * head_size],
                qkv[0, :, 2 * head_size :],
            )
        ]
    )
    mine = lax.all_to_all(attended, "sp", split_axis=1, concat_axis=2, tiled=True)
    piece = lax.all_gather(out_rows, "sp", axis=0, tiled=True)
    count = piece.shape[0]
    mixed = mine
    mixed = mixed.reshape(images, tok_local, count, head_size)
    contrib = jnp.einsum("itnc,ncd->itnd", mixed, piece, preferred_element_type=jnp.float32).astype(
        jnp.bfloat16
    )
    contrib = lax.optimization_barrier(contrib)
    total = jnp.sum(contrib.astype(jnp.float32), axis=2)
    return (gate[:, None, :] * total).astype(jnp.bfloat16)


def solution(mesh):
    placed = (P("grp", "sp", None), P("grp"), P(), P("sp", "grp", None), P("sp", "grp", None))
    return jax.shard_map(
        on_device, mesh=mesh, in_specs=placed, out_specs=P("grp", "sp", None), check_vma=False
    )
```

profile of v0, /device:TPU:0, one launch (start us, length us, event | category | flops | bytes accessed | tf_op | source)
XLA Modules:
  0.0 184.8 jit_solution(8514768617609309561)
XLA Ops:
  6.5 0.0 all-gather.6.cloned.1.call-start
  6.5 0.7 all-gather.6.cloned.1.call-update
  7.3 0.0 all-gather.4.cloned.1.call-start
  7.9 0.1 sine_convert_fusion
  8.0 1.3 convert_reduce_fusion.1
  9.4 1.5 fusion.6
  10.9 0.0 copy-start
  10.9 3.1 %fusion.25 = f32[1,9216]{1,0:T(1,128)S(1)} fusion(bf16[256,1]{0,1:T(2,128)(2,1)S(1)} %reshape.111, bf16[256,9216]{1,0:T(8,128)(2,1)} %param.7), kind=kOutput, calls=%fused_computation.37 | convolution fusion | flops 4718592 | bytes 4755968 | tf_op jit(solution)/shard_map/dot_general | solution.py:13
  14.0 0.0 copy-start.1
  14.0 0.0 copy-done
  14.0 1.3 fusion.9
  15.3 0.0 all-gather.4.cloned.1.call-update
  15.3 0.0 all-gather.8.cloned.1.call-start
  15.4 0.0 copy-done.1
  15.4 14.1 %all_gather.14 = bf16[1,128,3072]{2,1,0:T(8,128)(2,1)} all-gather(bf16[1,16,3072]{2,1,0:T(8,128)(2,1)S(1)} %copy-done.1), channel_id=1, replica_groups=mesh['grp'=8,'sp'=4] {'grp'}, dimensions={1}, use_global_device_ids=true | all-gather | bytes 884736 | tf_op jit(solution)/shard_map/all_gather | solution.py:59
  29.5 0.0 all-gather.8.cloned.1.call-update
  29.5 12.9 %all-gather.6.cloned.1.call-done = bf16[1,3072,384]{2,1,0:T(8,128)(2,1)} async-done(((bf16[1,384,384]{2,1,0:T(8,128)(2,1)}), bf16[1,3072,384]{2,1,0:T(8,128)(2,1)}) %all-gather.6.cloned.1.call-update) | async-done | bytes 2359312 | tf_op jit(solution)/shard_map/all_gather | solution.py:55
  42.4 65.0 %all-gather.4.cloned.1.call-done = bf16[1,512,3072]{2,1,0:T(8,128)(2,1)} async-done(((bf16[1,128,3072]{2,1,0:T(8,128)(2,1)}), bf16[1,512,3072]{2,1,0:T(8,128)(2,1)}) %all-gather.4.cloned.1.call-update) | async-done | bytes 3145744 | tf_op jit(solution)/shard_map/all_gather | solution.py:51
  107.4 4.4 %fusion.16 = bf16[1,512,384]{2,1,0:T(8,128)(2,1)S(1)} fusion(bf16[1,3072,384]{2,1,0:T(8,128)(2,1)} %all-gather.6.cloned.1.call-done, bf16[1,512,3072]{2,1,0:T(8,128)(2,1)} %all-gather.4.cloned.1.call-done), kind=kOutput, calls=%fused_computation.18 | convolution fusion | flops 1208156160 | bytes 5898240 | tf_op jit(solution)/shard_map/itc,cf->itf/dot_general | solution.py:52
  111.8 0.3 fusion.24
  112.1 0.2 fusion.22
  112.3 0.4 fusion.21
  112.7 0.2 copy.10
  112.9 0.5 broadcast.81
  113.5 1.4 reduce.3
  114.9 11.8 %all_to_all.15 = bf16[4,2,8192]{2,1,0:T(2,128)(2,1)S(1)} all-to-all(bf16[4,2,8192]{2,1,0:T(2,128)(2,1)S(1)} %reshape.113), channel_id=1, replica_groups=mesh['grp'=8,'sp'=4] {'sp'}, dimensions={0} | all-to-all | bytes 262144 | tf_op jit(solution)/shard_map/all_to_all | solution.py:69
  126.7 0.1 reshape.114
  126.8 47.0 %all-gather.8.cloned.1.call-done = bf16[4,128,3072]{2,1,0:T(8,128)(2,1)} async-done(((bf16[1,128,3072]{2,1,0:T(8,128)(2,1)}), bf16[4,128,3072]{2,1,0:T(8,128)(2,1)}) %all-gather.8.cloned.1.call-update) | async-done | bytes 3145744 | tf_op jit(solution)/shard_map/all_gather | solution.py:70
  173.8 2.9 %fusion = bf16[1,128,4,3072]{3,1,2,0:T(8,128)(2,1)S(1)} fusion(bf16[128,4,128]{2,0,1:T(8,128)(2,1)S(1)} %bitcast.61, bf16[4,128,3072]{2,1,0:T(8,128)(2,1)} %all-gather.8.cloned.1.call-done), kind=kOutput, calls=%fused_computation.2 | convolution fusion | flops 404226048 | bytes 6422528 | tf_op jit(solution)/shard_map/itnc,ncd->itnd/dot_general | solution.py:74
  176.7 0.6 convert_reduce_fusion
  177.3 1.0 fusion.10
  (7 shorter events, 0.1 us)
Async XLA Ops:
  6.5 35.9 %all-gather.6.cloned.1.call-start = ((), (), s32[]{:S(2)}) async-start(), calls=%async_computation.2 | async-start | bytes 2654208 | tf_op jit(solution)/shard_map/all_gather | solution.py:55
  7.3 100.2 %all-gather.4.cloned.1.call-start = ((), (), s32[]{:S(2)}) async-start(), calls=%async_computation.1 | async-start | bytes 3932160 | tf_op jit(solution)/shard_map/all_gather | solution.py:51
  10.9 3.2 %copy-start = (bf16[1,128,3072]{2,1,0:T(8,128)(2,1)S(1)}, bf16[1,128,3072]{2,1,0:T(8,128)(2,1)}, u32[]{:S(2)}) copy-start(bf16[1,128,3072]{2,1,0:T(8,128)(2,1)} %param.5) | copy-start | bytes 2359300
  14.0 1.4 copy-start.1
  15.3 158.5 %all-gather.8.cloned.1.call-start = ((), (), s32[]{:S(2)}) async-start(), calls=%async_computation.3 | async-start | bytes 3932160 | tf_op jit(solution)/shard_map/all_gather | solution.py:70
Sparse Core Ops, SparseCore 0:
  9.2 33.1 all-gather.5
  44.0 63.4 all-gather.3
  109.0 64.7 all-gather.7
where the time goes:
time: 185 us
  waiting for transfers between devices  126 us (68%)
  blocking collectives  25.8 us (14%)
  between operations  13.9 us (8%)
  matrix products  11.1 us (6%)
  other arithmetic  7.36 us (4%)
    all_gather x1, waiting for transfers between devices, on_device(): whole = lax.all_gather(normed, 'sp', axis=1, tiled=True)  65 us
    all_gather x1, waiting for transfers between devices, on_device(): piece = lax.all_gather(out_rows, 'sp', axis=0, tiled=True)  47 us
    all_gather x1, blocking collectives, on_device(): out_rows = lax.all_gather(w_out, 'grp', axis=1, tiled=True)  14.1 us
    all_gather x1, waiting for transfers between devices, on_device(): lax.all_gather(w_qkv, 'grp', axis=1, tiled=True)[0]  12.9 us
    all_to_all x1, blocking collectives, on_device(): lax.all_to_all(attended, 'sp', split_axis=1, concat_axis=2, tiled=True)  11.8 us
    dot_general x1, matrix products, on_device(): jnp.einsum('itc,cf->itf', whole, lax.all_gather(w_qkv, 'grp', axis=1, til...  4.41 us
  transfers between devices with their start and end apart: 3, of which 3 were waited for; matrix products, arithmetic and copies ran while one was open for 8% of the time, Pallas kernels for 0%

commit v1 on v0

--- a/solution.py
+++ b/solution.py
@@ -48,7 +48,7 @@
     scale = mod[:, width : 2 * width]
     gate = mod[:, 2 * width :]
     normed = normalize(latents, shift, scale)
-    whole = lax.all_gather(normed, "sp", axis=1, tiled=True)
+    whole = jnp.concatenate(lax.all_gather(normed, "sp"), axis=1)
     qkv_sum = jnp.einsum(
         "itc,cf->itf",
         whole,

time: 185 us -> 185 us (level)
  no operation moved by 1% of the time
where the time goes in v1:
time: 185 us
  waiting for transfers between devices  126 us (68%)
  blocking collectives  25.8 us (14%)
  between operations  13.9 us (8%)
  matrix products  11.1 us (6%)
  other arithmetic  7.34 us (4%)
    all_gather x1, waiting for transfers between devices, on_device(): whole = jnp.concatenate(lax.all_gather(normed, 'sp'), axis=1)  65 us
    all_gather x1, waiting for transfers between devices, on_device(): piece = lax.all_gather(out_rows, 'sp', axis=0, tiled=True)  47 us
    all_gather x1, blocking collectives, on_device(): out_rows = lax.all_gather(w_out, 'grp', axis=1, tiled=True)  14.1 us
    all_gather x1, waiting for transfers between devices, on_device(): lax.all_gather(w_qkv, 'grp', axis=1, tiled=True)[0]  12.9 us
    all_to_all x1, blocking collectives, on_device(): lax.all_to_all(attended, 'sp', split_axis=1, concat_axis=2, tiled=True)  11.8 us
    dot_general x1, matrix products, on_device(): jnp.einsum('itc,cf->itf', whole, lax.all_gather(w_qkv, 'grp', axis=1, til...  4.4 us
  transfers between devices with their start and end apart: 3, of which 3 were waited for; matrix products, arithmetic and copies ran while one was open for 8% of the time, Pallas kernels for 0%

profile of v1, /device:TPU:0, one launch (start us, length us, event | category | flops | bytes accessed | tf_op | source)
XLA Modules:
  0.0 184.8 jit_solution(15497897379941692640)
XLA Ops:
  6.5 0.0 all-gather.5.cloned.1.call-start
  6.5 0.7 all-gather.5.cloned.1.call-update
  7.3 0.0 all-gather.9.cloned.1.call-start
  7.9 0.1 sine_convert_fusion
  8.0 1.3 convert_reduce_fusion.1
  9.4 1.5 fusion.5
  10.9 0.0 copy-start
  10.9 3.1 %fusion.20 = f32[1,9216]{1,0:T(1,128)S(1)} fusion(bf16[256,1]{0,1:T(2,128)(2,1)S(1)} %reshape.115, bf16[256,9216]{1,0:T(8,128)(2,1)} %param.7), kind=kOutput, calls=%fused_computation.36 | convolution fusion | flops 4718592 | bytes 4755968 | tf_op jit(solution)/shard_map/dot_general | solution.py:13
  14.0 0.0 copy-start.1
  14.0 0.0 copy-done
  14.0 1.3 fusion.8
  15.3 0.0 all-gather.9.cloned.1.call-update
  15.3 0.0 all-gather.7.cloned.1.call-start
  15.4 0.0 copy-done.1
  15.4 14.1 %all_gather.18 = bf16[1,128,3072]{2,1,0:T(8,128)(2,1)} all-gather(bf16[1,16,3072]{2,1,0:T(8,128)(2,1)S(1)} %copy-done.1), channel_id=1, replica_groups=mesh['grp'=8,'sp'=4] {'grp'}, dimensions={1}, use_global_device_ids=true | all-gather | bytes 884736 | tf_op jit(solution)/shard_map/all_gather | solution.py:59
  29.5 0.0 all-gather.7.cloned.1.call-update
  29.5 12.9 %all-gather.5.cloned.1.call-done = bf16[1,3072,384]{2,1,0:T(8,128)(2,1)} async-done(((bf16[1,384,384]{2,1,0:T(8,128)(2,1)}), bf16[1,3072,384]{2,1,0:T(8,128)(2,1)}) %all-gather.5.cloned.1.call-update) | async-done | bytes 2359312 | tf_op jit(solution)/shard_map/all_gather | solution.py:55
  42.4 65.0 %all-gather.9.cloned.1.call-done = bf16[4,128,3072]{2,1,0:T(8,128)(2,1)} async-done(((bf16[1,128,3072]{2,1,0:T(8,128)(2,1)}), bf16[4,128,3072]{2,1,0:T(8,128)(2,1)}) %all-gather.9.cloned.1.call-update) | async-done | bytes 3145744 | tf_op jit(solution)/shard_map/all_gather | solution.py:51
  107.4 4.4 %fusion.13 = bf16[1,512,384]{2,1,0:T(8,128)(2,1)S(1)} fusion(bf16[512,3072]{1,0:T(8,128)(2,1)} %bitcast.60, bf16[1,3072,384]{2,1,0:T(8,128)(2,1)} %all-gather.5.cloned.1.call-done), kind=kOutput, calls=%fused_computation.17 | convolution fusion | flops 1208156160 | bytes 5898240 | tf_op jit(solution)/shard_map/itc,cf->itf/dot_general | solution.py:52
  111.8 0.3 fusion.19
  112.2 0.2 fusion.17
  112.4 0.4 fusion.16
  112.7 0.2 copy.10
  113.0 0.5 broadcast.81
  113.5 1.4 reduce.3
  114.9 11.8 %all_to_all.15 = bf16[4,2,8192]{2,1,0:T(2,128)(2,1)S(1)} all-to-all(bf16[4,2,8192]{2,1,0:T(2,128)(2,1)S(1)} %reshape.117), channel_id=1, replica_groups=mesh['grp'=8,'sp'=4] {'sp'}, dimensions={0} | all-to-all | bytes 262144 | tf_op jit(solution)/shard_map/all_to_all | solution.py:69
  126.7 0.1 reshape.118
  126.8 47.0 %all-gather.7.cloned.1.call-done = bf16[4,128,3072]{2,1,0:T(8,128)(2,1)} async-done(((bf16[1,128,3072]{2,1,0:T(8,128)(2,1)}), bf16[4,128,3072]{2,1,0:T(8,128)(2,1)}) %all-gather.7.cloned.1.call-update) | async-done | bytes 3145744 | tf_op jit(solution)/shard_map/all_gather | solution.py:70
  173.9 2.9 %fusion = bf16[1,128,4,3072]{3,1,2,0:T(8,128)(2,1)S(1)} fusion(bf16[128,4,128]{2,0,1:T(8,128)(2,1)S(1)} %bitcast.56, bf16[4,128,3072]{2,1,0:T(8,128)(2,1)} %all-gather.7.cloned.1.call-done), kind=kOutput, calls=%fused_computation.2 | convolution fusion | flops 404226048 | bytes 6422528 | tf_op jit(solution)/shard_map/itnc,ncd->itnd/dot_general | solution.py:74
  176.7 0.6 convert_reduce_fusion
  177.3 1.0 fusion.9
  (7 shorter events, 0.1 us)
Async XLA Ops:
  6.5 35.9 %all-gather.5.cloned.1.call-start = ((), (), s32[]{:S(2)}) async-start(), calls=%async_computation.1 | async-start | bytes 2654208 | tf_op jit(solution)/shard_map/all_gather | solution.py:55
  7.3 100.2 %all-gather.9.cloned.1.call-start = ((), (), s32[]{:S(2)}) async-start(), calls=%async_computation.3 | async-start | bytes 3932160 | tf_op jit(solution)/shard_map/all_gather | solution.py:51
  10.9 3.2 %copy-start = (bf16[1,128,3072]{2,1,0:T(8,128)(2,1)S(1)}, bf16[1,128,3072]{2,1,0:T(8,128)(2,1)}, u32[]{:S(2)}) copy-start(bf16[1,128,3072]{2,1,0:T(8,128)(2,1)} %param.5) | copy-start | bytes 2359300
  14.0 1.4 copy-start.1
  15.3 158.5 %all-gather.7.cloned.1.call-start = ((), (), s32[]{:S(2)}) async-start(), calls=%async_computation.2 | async-start | bytes 3932160 | tf_op jit(solution)/shard_map/all_gather | solution.py:70
Sparse Core Ops, SparseCore 0:
  9.2 33.1 all-gather.4
  44.0 63.4 all-gather.8
  109.0 64.7 all-gather.6
